TPU v7x, 32 devices: a whole 2x2x4 slice. The times are simulated.
32 devices in a mesh: chain: 8 (over y, x, core), col: 4 (over z).
Axes of the slice: x: 2, y: 2, z: 4, core: 2. Of those that a mesh axis runs over, the one named last changes fastest.
Arguments:
- rhs: bfloat16 [16, 64, 2560], P('chain', None, 'col'), may hold values from -6 to 6
- block_inverse: bfloat16 [16, 2560, 2560], P('chain', 'col'), as said below
- entry_factor: bfloat16 [16, 2560, 128], P('chain', 'col'), as said below
- exit_factor: bfloat16 [16, 2560, 128], P('chain', 'col'), as said below
- previous: bfloat16 [64, 2560], P(None, 'col'), may hold values from -6 to 6
Outputs:
- solution: float32 [16, 64, 2560], P('chain', None, 'col')
Inputs may be any that keep to these rules, and one draw needn't show every extreme that they name: Every block of block_inverse equals its own transpose. `entry_factor`: entries are independent, of mean zero. `exit_factor`: entries are independent, of mean zero.
All inputs are finite; a program needn't handle non-finite values.
Results may differ from a plain program's by a relative error of at most 0.0003.
Values may be sent and summed in bfloat16 or wider, within the bound.
A program may use at most 64 MiB of HBM per device.

v0:
```python
import jax
import jax.numpy as jnp
from jax import lax
from jax.sharding import PartitionSpec as P


def from_behind(block, axis, distance):
    devices = range(lax.axis_size(axis))
    route = [(i - distance, i) for i in devices if i - distance in devices]
    return lax.ppermute(block, axis, route)


def entering(part, axis, combine, identity, reverse):
    count = lax.axis_size(axis)
    place = lax.axis_index(axis)
    ahead = count - 1 - place if reverse else place
    gathered = jax.tree.map(lambda a: lax.all_gather(a, axis), part)
    state = jax.tree.map(lambda a, e: jnp.zeros_like(a) + jnp.asarray(e, a.dtype), part, identity)

    def one(step, state):
        source = count - 1 - step if reverse else step
        return combine(
            state, jax.tree.map(lambda a: lax.dynamic_index_in_dim(a, source, 0, False), gathered)
        )

    return lax.fori_loop(0, ahead, one, state)


def compose(earlier, later):
    exact = lax.Precision.HIGHEST
    first_map, first_shift = earlier
    second_map, second_shift = later
    return (
        jnp.dot(first_map, second_map, precision=exact),
        jnp.dot(first_shift, second_map, precision=exact) + second_shift,
    )


def shards(rhs, block_inverse, entry_factor, exit_factor, previous):
    exact = lax.Precision.HIGHEST
    intervals_here = rhs.shape[0]
    column_count = rhs.shape[1]
    state_width = entry_factor.shape[2]
    arriving = from_behind(exit_factor[:1], "chain", -1)
    following = jnp.concatenate([exit_factor[1:], arriving], axis=0)
    couple_part = -jnp.einsum(
        "irn,irm->inm", entry_factor, following, preferred_element_type=jnp.float32
    )
    source_part = jnp.einsum("icr,irm->icm", rhs, following, preferred_element_type=jnp.float32)
    opening_part = jnp.dot(previous, exit_factor[0], preferred_element_type=jnp.float32)
    couple, source, opening = lax.psum((couple_part, source_part, opening_part), "col")
    identity = jnp.eye(state_width, dtype=jnp.float32)
    empty_shift = jnp.zeros((column_count, state_width), jnp.float32)
    first_chain = lax.axis_index("chain") == 0
    matrix = identity
    offset = empty_shift
    for position in range(intervals_here):
        matrix = jnp.dot(matrix, couple[position], precision=exact)
        offset = jnp.dot(offset, couple[position], precision=exact) + source[position]
    folded = jnp.dot(opening, matrix, precision=exact) + offset
    offset = jnp.where(first_chain, folded, offset)
    matrix = jnp.where(first_chain, jnp.zeros_like(matrix), matrix)
    _, incoming = entering((matrix, offset), "chain", compose, (identity, empty_shift), False)
    carry_state = jnp.where(first_chain, opening, incoming)
    solved_list = []
    for position in range(intervals_here):
        solved_list.append(
            rhs[position].astype(jnp.float32)
            - jnp.dot(carry_state, entry_factor[position].astype(jnp.float32).T, precision=exact)
        )
        carry_state = jnp.dot(carry_state, couple[position], precision=exact) + source[position]
    forward = jnp.stack(solved_list).astype(jnp.bfloat16)
    applied = jnp.einsum(
        "icb,irb->icr",
        lax.all_gather(forward, "col", axis=2, tiled=True),
        block_inverse,
        preferred_element_type=jnp.float32,
    )
    carried_part = jnp.einsum(
        "icr,irn->icn",
        applied.astype(jnp.bfloat16),
        entry_factor,
        preferred_element_type=jnp.float32,
    )
    carried = lax.psum(carried_part, "col")
    last_chain = lax.axis_index("chain") == lax.axis_size("chain") - 1
    matrix = identity
    offset = empty_shift
    for position in reversed(range(intervals_here)):
        turned = couple[position].T
        matrix = jnp.dot(matrix, turned, precision=exact)
        offset = jnp.dot(offset, turned, precision=exact) + carried[position]
    matrix = jnp.where(last_chain, jnp.zeros_like(matrix), matrix)
    _, behind = entering((matrix, offset), "chain", compose, (identity, empty_shift), True)
    results = [None] * intervals_here
    for position in reversed(range(intervals_here)):
        results[position] = applied[position] - jnp.dot(
            behind, following[position].astype(jnp.float32).T, precision=exact
        )
        behind = jnp.dot(behind, couple[position].T, precision=exact) + carried[position]
    return jnp.stack(results)


def solution(mesh):
    placed = (
        P("chain", None, "col"),
        P("chain", "col", None),
        P("chain", "col", None),
        P("chain", "col", None),
        P(None, "col"),
    )
    return jax.shard_map(
        shards, mesh=mesh, in_specs=placed, out_specs=P("chain", None, "col"), check_vma=False
    )
```

profile of v0, /device:TPU:0, one launch (start us, length us, event | category | flops | bytes accessed | tf_op | source)
XLA Modules:
  0.0 161.5 jit_solution(1179635024437629665)
XLA Ops:
  6.5 1.1 fusion.37
  7.8 1.3 collective-permute-start
  9.3 1.8 %collective-permute-done = bf16[1,640,128]{1,2,0:T(8,128)(2,1)S(1)} collective-permute-done((bf16[1,640,128]{1,2,0:T(8,128)(2,1)S(1)}, bf16[1,640,128]{1,2,0:T(8,128)(2,1)S(1)}, u32[]{:S(2)}, u32[]{:S(2)}) %collective-permute-start) | collective-permute-done | bytes 163872 | tf_op jit(solution)/shard_map/ppermute | solution.py:10
  11.1 1.8 %convolution_bitcast_fusion.2 = f32[2,64,128]{2,1,0:T(8,128)} fusion(bf16[2,64,640]{2,1,0:T(8,128)(2,1)} %param.9, bf16[1,640,128]{1,2,0:T(8,128)(2,1)S(1)} %collective-permute-done, bf16[1,640,128]{1,2,0:T(8,128)(2,1)S(1)} %copy.11), kind=kOutput, calls=%fused_computation.23 | convolution fusion | flops 21135360 | bytes 557056 | tf_op jit(solution)/shard_map/icr,irm->icm/dot_general | solution.py:49
  12.9 1.9 %fusion.10 = f32[2,128,128]{1,2,0:T(8,128)} fusion(bf16[2,640,128]{2,1,0:T(8,128)(2,1)} %param.11, bf16[1,640,128]{1,2,0:T(8,128)(2,1)S(1)} %collective-permute-done, bf16[1,640,128]{1,2,0:T(8,128)(2,1)S(1)} %copy.11), kind=kOutput, calls=%fused_computation.17 | convolution fusion | flops 42139648 | bytes 786432 | tf_op jit(solution)/shard_map/irn,irm->inm/dot_general | solution.py:46
  14.8 1.1 fusion.17
  15.9 21.0 %psum.28 = f32[64,128]{1,0:T(8,128)S(1)} all-reduce(f32[64,128]{1,0:T(8,128)S(1)} %fusion.17), channel_id=1, replica_groups=mesh['chain'=8,'col'=4] {'col'}, use_global_device_ids=true, to_apply=%region_0.0 | all-reduce | flops 8192 | bytes 65536 | tf_op jit(solution)/shard_map/psum | solution.py:51
  36.9 18.5 %all-reduce.6.cloned.1.call-done = (f32[2,128,128]{1,2,0:T(8,128)}, f32[2,64,128]{2,1,0:T(8,128)}) async-done(((f32[2,128,128]{1,2,0:T(8,128)}, f32[2,64,128]{2,1,0:T(8,128)}), (f32[2,128,128]{1,2,0:T(8,128)}, f32[2,64,128]{2,1,0:T(8,128)})) %all-reduce.6.cloned.1.call-update) | async-done | bytes 196624 | tf_op jit(solution)/shard_map/psum | solution.py:51
  55.4 1.1 fusion.27
  56.5 1.1 convolution_add_fusion.5
  57.6 1.1 convolution_add_fusion.4
  58.7 1.1 broadcast_select_fusion
  60.0 9.2 %all-gather.1 = f32[512,128]{1,0:T(8,128)S(1)} all-gather(f32[64,128]{1,0:T(8,128)S(1)} %fusion.15), channel_id=3, replica_groups=mesh['chain'=8,'col'=4] {'chain'}, dimensions={0}, use_global_device_ids=true | all-gather | bytes 294912 | tf_op jit(solution)/shard_map/all_gather | solution.py:17
  69.2 9.8 %all-gather = f32[1024,128]{1,0:T(8,128)S(1)} all-gather(f32[128,128]{1,0:T(8,128)S(1)} %get-tuple-element.159), channel_id=2, replica_groups=mesh['chain'=8,'col'=4] {'chain'}, dimensions={0}, use_global_device_ids=true | all-gather | bytes 589824 | tf_op jit(solution)/shard_map/all_gather | solution.py:17
  79.3 1.1 convolution_add_fusion.3
  80.5 1.0 fusion.26
  81.9 17.2 %all_gather.31 = bf16[2,64,2560]{2,1,0:T(8,128)(2,1)S(1)} all-gather(bf16[2,64,640]{2,1,0:T(8,128)(2,1)S(1)} %pad_maximum_fusion.4), channel_id=1, replica_groups=mesh['chain'=8,'col'=4] {'col'}, dimensions={2}, use_global_device_ids=true | all-gather | bytes 819200 | tf_op jit(solution)/shard_map/all_gather | solution.py:75
  99.1 4.9 %fusion.38 = f32[2,64,640]{2,1,0:T(8,128)S(1)} fusion(bf16[2,64,2560]{2,1,0:T(8,128)(2,1)S(1)} %all_gather.31, bf16[2,640,2560]{2,1,0:T(8,128)(2,1)} %param.10), kind=kOutput, calls=%fused_computation.68 | convolution fusion | flops 419430400 | bytes 7536640 | tf_op jit(solution)/shard_map/icb,irb->icr/dot_general | solution.py:73
  105.1 9.9 %all-gather.2 = f32[1024,128]{1,0:T(8,128)S(1)} all-gather(f32[128,128]{1,0:T(8,128)S(1)} %convolution_select_fusion), channel_id=4, replica_groups=mesh['chain'=8,'col'=4] {'chain'}, dimensions={0}, use_global_device_ids=true | all-gather | bytes 589824 | tf_op jit(solution)/shard_map/all_gather | solution.py:17
  115.0 24.6 %all-reduce.4.cloned.1.call-done = f32[2,64,128]{2,1,0:T(8,128)} async-done(((f32[2,64,128]{2,1,0:T(8,128)}), f32[2,64,128]{2,1,0:T(8,128)}) %all-reduce.4.cloned.1.call-update) | async-done | bytes 65552 | tf_op jit(solution)/shard_map/psum | solution.py:85
  140.5 0.9 convolution_add_fusion.1
  141.5 9.3 %all-gather.3 = f32[512,128]{1,0:T(8,128)S(1)} all-gather(f32[64,128]{1,0:T(8,128)S(1)} %convolution_add_fusion.1), channel_id=5, replica_groups=mesh['chain'=8,'col'=4] {'chain'}, dimensions={0}, use_global_device_ids=true | all-gather | bytes 294912 | tf_op jit(solution)/shard_map/all_gather | solution.py:17
  150.8 1.6 %while.27 = (s32[]{:T(128)}, f32[64,128]{1,0:T(8,128)S(1)}, s32[]{:T(128)}, f32[8,128,128]{2,1,0:T(8,128)S(1)}, f32[8,64,128]{2,1,0:T(8,128)S(1)}, /*index=5*/s32[]{:T(128)}, s32[]{:T(128)}, s32[]{:T(128)}, s32[]{:T(128)}) while((s32[]{:T(128)}, f32[64,128]{1,0:T(8,128)S(1)}, s32[]{:T(128)}, f32[8,128,128]{2,1,0:T(8,128)S(1)}, ...), condition=%wide.region_7.8_spmd, body=%wide.region_6.7_spmd.sunk | while | flops 12591110 | bytes 230539 | solution.py:26
  152.4 0.9 convolution_add_fusion
  (43 shorter events, 5.9 us)
Async XLA Ops:
  6.5 8.3 %copy-start = (bf16[64,640]{1,0:T(8,128)(2,1)S(1)}, bf16[64,640]{1,0:T(8,128)(2,1)}, u32[]{:S(2)}) copy-start(bf16[64,640]{1,0:T(8,128)(2,1)} %param.13) | copy-start | bytes 245764
  6.5 72.5 %copy-start.4 = (bf16[2,64,640]{2,1,0:T(8,128)(2,1)S(1)}, bf16[2,64,640]{2,1,0:T(8,128)(2,1)}, u32[]{:S(2)}) copy-start(bf16[2,64,640]{2,1,0:T(8,128)(2,1)} %param.9) | copy-start | bytes 491524
  6.5 72.5 %copy-start.2 = (bf16[2,640,128]{2,1,0:T(8,128)(2,1)S(1)}, bf16[2,640,128]{2,1,0:T(8,128)(2,1)}, u32[]{:S(2)}) copy-start(bf16[2,640,128]{2,1,0:T(8,128)(2,1)} %param.11) | copy-start | bytes 983044
  6.5 48.9 %all-reduce.6.cloned.1.call-start = ((), (), s32[]{:S(2)}) async-start(), calls=%async_computation.1 | async-start | bytes 393216 | tf_op jit(solution)/shard_map/psum | solution.py:51
  7.8 3.3 %collective-permute-start = (bf16[1,640,128]{1,2,0:T(8,128)(2,1)S(1)}, bf16[1,640,128]{1,2,0:T(8,128)(2,1)S(1)}, u32[]{:S(2)}, u32[]{:S(2)}) collective-permute-start(bf16[1,640,128]{1,2,0:T(8,128)(2,1)S(1)} %copy.10), channel_id=1, source_target_pairs={{4,0},{8,4},{12,8},{16,12},{20,16},{24,20},{28,24},{5,1},{9,5},{13... | collective-permute-start | bytes 491528 | tf_op jit(solution)/shard_map/ppermute | solution.py:10
  14.8 124.8 %all-reduce.4.cloned.1.call-start = ((), (), s32[]{:S(2)}) async-start(), calls=%async_computation | async-start | bytes 131072 | tf_op jit(solution)/shard_map/psum | solution.py:85
  59.8 45.1 %copy-start.1 = (f32[2,128,128]{1,2,0:T(8,128)S(1)}, f32[2,128,128]{1,2,0:T(8,128)}, u32[]{:S(2)}) copy-start(f32[2,128,128]{1,2,0:T(8,128)} %get-tuple-element.155) | copy-start | bytes 393220
  79.3 74.0 %copy-start.3 = (bf16[2,640,128]{2,1,0:T(8,128)(2,1)S(1)}, bf16[2,640,128]{2,1,0:T(8,128)(2,1)}, u32[]{:S(2)}) copy-start(bf16[2,640,128]{2,1,0:T(8,128)(2,1)} %param.12) | copy-start | bytes 983044
Sparse Core Ops, SparseCore 0:
  14.9 40.4 all-reduce.5
  105.0 34.5 all-reduce.3
where the time goes:
time: 162 us; the launch traced here: 161 us
  blocking collectives  76.4 us (47%)
  waiting for transfers between devices  45 us (28%)
  matrix products  22.7 us (14%)
  between operations  13.6 us (8%)
    all_gather x4, blocking collectives, entering(): gathered = jax.tree.map(lambda a: lax.all_gather(a, axis), part)  38.2 us
    psum x1, waiting for transfers between devices, shards(): carried = lax.psum(carried_part, 'col')  24.6 us
    psum x1, blocking collectives, shards(): lax.psum((couple_part, source_part, opening_part), 'col')  21 us
    psum x1, waiting for transfers between devices, shards(): lax.psum((couple_part, source_part, opening_part), 'col')  18.5 us
    all_gather x1, blocking collectives, shards(): lax.all_gather(forward, 'col', axis=2, tiled=True)  17.2 us
    dot_general x1, matrix products, shards(): jnp.einsum('icb,irb->icr', lax.all_gather(forward, 'col', axis=2, tiled=T...  4.94 us
  transfers between devices with their start and end apart: 3, of which 3 were waited for; matrix products, arithmetic and copies ran while one was open for 1% of the time, Pallas kernels for 0%

commit v1 on v0

v1 whole, which is shorter than its diff:
```python
import functools

import jax
import jax.numpy as jnp
from jax import lax
from jax.experimental import pallas as pl
from jax.experimental.pallas import tpu as pltpu
from jax.sharding import PartitionSpec as P

MESH = pl.DeviceIdType.MESH
F32 = jnp.float32
BF16 = jnp.bfloat16


def dot_t(a, b):
    return lax.dot_general(a, b, (((1,), (1,)), ((), ())), preferred_element_type=F32)


def terms(x):
    first = x.astype(BF16)
    rest = x - first.astype(F32)
    second = rest.astype(BF16)
    third = (rest - second.astype(F32)).astype(BF16)
    return first, second, third


def split_dot_t(x, low):
    rows = x.shape[0]
    product = dot_t(jnp.concatenate(terms(x), axis=0), low)
    return (product[2 * rows:] + product[rows:2 * rows]) + product[:rows]


def wide_dot(a, b, dot):
    rows = a.shape[0]
    a1, a2, a3 = terms(a)
    b1, b2, b3 = terms(b)
    p1 = dot(jnp.concatenate([a1, a2, a3], axis=0), b1)
    p2 = dot(jnp.concatenate([a1, a2], axis=0), b2)
    p3 = dot(a1, b3)
    small = (p1[2 * rows:] + p2[rows:]) + p3
    return (small + (p1[rows:2 * rows] + p2[:rows])) + p1[:rows]


def plain_dot(a, b):
    return jnp.dot(a, b, preferred_element_type=F32)


def exact_dot(a, b):
    return wide_dot(a, b, plain_dot)


def exact_dot_t(a, b):
    return wide_dot(a, b, dot_t)


def kernel(
    n, m, rhs_hbm, binv_hbm, entry_hbm, exit_hbm, prev_hbm, out_ref,
    rhs, binv, entry, exits, prev, arriving,
    parts, parts_in, opening, opening_in, summed, comp, gathered,
    states, forward, applied, carried, carried_in, carried_sum, back, back_in, behind,
    local_sem, exit_sem, part_send, part_recv, open_send, open_recv,
    comp_send, comp_recv, state_send, state_recv, fwd_send, fwd_recv,
    car_send, car_recv, back_send, back_recv, beh_send, beh_recv,
):
    c = lax.axis_index("chain")
    k = lax.axis_index("col")
    count, columns, width = rhs.shape
    nx = entry.shape[2]

    def owner_of(chain):
        return m // 2 - 1 + lax.rem(chain, 2)

    owner = owner_of(c)
    is_owner = k == owner
    unsent = []

    def remote(src, dst, send, recv, where):
        return pltpu.make_async_remote_copy(
            src_ref=src, dst_ref=dst, send_sem=send, recv_sem=recv,
            device_id=where, device_id_type=MESH,
        )

    def send(condition, *args):
        @pl.when(condition)
        def _():
            remote(*args).start()

        unsent.append((condition, args))

    loads = [
        pltpu.make_async_copy(exit_hbm, exits, local_sem.at[0]),
        pltpu.make_async_copy(entry_hbm, entry, local_sem.at[1]),
        pltpu.make_async_copy(rhs_hbm, rhs, local_sem.at[2]),
        pltpu.make_async_copy(prev_hbm, prev, local_sem.at[3]),
    ] + [
        pltpu.make_async_copy(binv_hbm.at[p], binv.at[p], local_sem.at[4 + p])
        for p in range(count)
    ]
    for load in loads:
        load.start()

    barrier = pltpu.get_barrier_semaphore()
    for d in range(1, m):
        pl.semaphore_signal(
            barrier, 1, device_id={"col": lax.rem(k + d, m)}, device_id_type=MESH
        )

    @pl.when(c > 0)
    def _():
        pl.semaphore_signal(barrier, 1, device_id={"chain": c - 1}, device_id_type=MESH)

    @pl.when(c < n - 1)
    def _():
        pl.semaphore_signal(barrier, 1, device_id={"chain": c + 1}, device_id_type=MESH)

    @pl.when(is_owner)
    def _():
        for d in range(1, n):
            other = lax.rem(c + d, n)
            pl.semaphore_signal(
                barrier, 1, device_id={"chain": other, "col": owner_of(other)},
                device_id_type=MESH,
            )

    @pl.when(c == n - 1)
    def _():
        arriving[...] = jnp.zeros_like(arriving)

    expected = m - 1 + jnp.where(c > 0, 1, 0) + jnp.where(c < n - 1, 1, 0)
    pl.semaphore_wait(barrier, expected + jnp.where(is_owner, n - 1, 0))

    loads[0].wait()
    send(c > 0, exits.at[0], arriving, exit_sem.at[0], exit_sem.at[1], {"chain": c - 1})
    for load in loads[1:4]:
        load.wait()

    @pl.when(c == 0)
    def _():
        opening[...] = jnp.dot(prev[...], exits[0], preferred_element_type=F32)

    send(
        (c == 0) & jnp.logical_not(is_owner), opening, opening_in.at[k],
        open_send, open_recv.at[k], {"col": owner},
    )

    def following(p):
        return exits[p + 1] if p + 1 < count else arriving[...]

    for p in range(count):
        if p + 1 == count:
            @pl.when(c < n - 1)
            def _():
                remote(
                    exits.at[0], arriving, exit_sem.at[0], exit_sem.at[1], {"chain": c}
                ).wait_recv()
        parts[p, :nx] = -lax.dot_general(
            entry[p], following(p), (((0,), (0,)), ((), ())), preferred_element_type=F32
        )
        parts[p, nx:] = jnp.dot(rhs[p], following(p), preferred_element_type=F32)
        send(
            jnp.logical_not(is_owner), parts.at[p], parts_in.at[k, p],
            part_send.at[p], part_recv.at[k, p], {"col": owner},
        )

    def spread(buffer, p, sends, recvs):
        for d in range(1, m):
            send(
                is_owner, buffer.at[p], buffer.at[p], sends.at[p, d - 1], recvs.at[p],
                {"col": lax.rem(k + d, m)},
            )

    @pl.when(is_owner)
    def _():
        for p in range(count):
            for d in range(1, m):
                other = lax.rem(k + d, m)
                remote(
                    parts.at[p], parts_in.at[other, p], part_send.at[p],
                    part_recv.at[other, p], {"col": other},
                ).wait_recv()
            total = parts[p]
            for d in range(1, m):
                total += parts_in[lax.rem(k + d, m), p]
            summed[p] = total
        both = summed[0]
        for p in range(1, count):
            both = exact_dot(both, summed[p, :nx])
            both = jnp.concatenate([both[:nx], both[nx:] + summed[p, nx:]], axis=0)
        comp[...] = both

        @pl.when(c == 0)
        def _():
            total = opening[...]
            for d in range(1, m):
                other = lax.rem(k + d, m)
                remote(
                    opening, opening_in.at[other], open_send,
                    open_recv.at[other], {"col": other},
                ).wait_recv()
                total += opening_in[other]
            states[0] = total
            comp[nx:] = exact_dot(total, comp[:nx]) + comp[nx:]

    for d in range(1, n):
        later = lax.rem(c + d, n)
        send(
            is_owner & (c + d < n), comp, gathered.at[c], comp_send.at[d - 1],
            comp_recv.at[c], {"chain": later, "col": owner_of(later)},
        )
    for d in range(1, n):
        earlier = lax.rem(c - d + n, n)
        send(
            is_owner & (c - d >= 0), comp.at[pl.ds(0, nx)], gathered.at[c, pl.ds(0, nx)],
            comp_send.at[n - 1 + d - 1], comp_recv.at[c],
            {"chain": earlier, "col": owner_of(earlier)},
        )

    @pl.when(is_owner & (c > 0))
    def _():
        def fold(s, state):
            remote(
                comp, gathered.at[s], comp_send.at[0], comp_recv.at[s], {"chain": c}
            ).wait_recv()
            return exact_dot(state, gathered[s, :nx]) + gathered[s, nx:]

        states[0] = lax.fori_loop(0, c, fold, jnp.zeros((columns, nx), F32))

    for p in range(count):
        if p > 0:
            @pl.when(is_owner)
            def _():
                states[p] = exact_dot(states[p - 1], summed[p - 1, :nx]) + summed[p - 1, nx:]
        spread(states, p, state_send, state_recv)

    for p in range(count):
        @pl.when(jnp.logical_not(is_owner))
        def _():
            remote(
                states.at[p], states.at[p], state_send.at[p, 0], state_recv.at[p], {"col": k}
            ).wait_recv()
        forward[k, p] = (
            rhs[p].astype(F32) - split_dot_t(states[p], entry[p])
        ).astype(BF16)
        for way, step in ((0, 1), (1, -1)):
            beyond = k + step
            send(
                (beyond >= 0) & (beyond < m), forward.at[k, p], forward.at[k, p],
                fwd_send.at[k, p, way], fwd_recv.at[k, p], {"col": beyond},
            )

    def block(j, p):
        return binv[p, :, pl.ds(pl.multiple_of(j * width, 128), width)]

    for p in range(count):
        loads[4 + p].wait()
        applied[p] = dot_t(forward[k, p], block(k, p))
    for d in range(1, m):
        for p in range(count):
            for way, step in ((0, 1), (1, -1)):
                j = k - step * d
                beyond = k + step
                there = (j >= 0) & (j < m)

                @pl.when(there)
                def _():
                    remote(
                        forward.at[j, p], forward.at[j, p], fwd_send.at[j, p, way],
                        fwd_recv.at[j, p], {"col": j},
                    ).wait_recv()

                send(
                    there & (beyond >= 0) & (beyond < m), forward.at[j, p], forward.at[j, p],
                    fwd_send.at[j, p, way], fwd_recv.at[j, p], {"col": beyond},
                )

                @pl.when(there)
                def _():
                    applied[p] += dot_t(forward[j, p], block(j, p))

    for p in reversed(range(count)):
        carried[p] = jnp.dot(applied[p].astype(BF16), entry[p], preferred_element_type=F32)
        send(
            jnp.logical_not(is_owner), carried.at[p], carried_in.at[k, p],
            car_send.at[p], car_recv.at[k, p], {"col": owner},
        )

    @pl.when(is_owner)
    def _():
        offset = None
        for p in reversed(range(count)):
            total = carried[p]
            for d in range(1, m):
                other = lax.rem(k + d, m)
                remote(
                    carried.at[p], carried_in.at[other, p], car_send.at[p],
                    car_recv.at[other, p], {"col": other},
                ).wait_recv()
                total += carried_in[other, p]
            carried_sum[p] = total
            if offset is None:
                offset = total
            else:
                offset = exact_dot_t(offset, summed[p, :nx]) + total
        back[...] = offset

    for d in range(1, n):
        earlier = lax.rem(c - d + n, n)
        send(
            is_owner & (c - d >= 0), back, back_in.at[c], back_send.at[d - 1],
            back_recv.at[c], {"chain": earlier, "col": owner_of(earlier)},
        )

    @pl.when(is_owner)
    def _():
        def fold(i, state):
            s = n - 1 - i
            remote(
                comp.at[pl.ds(0, nx)], gathered.at[s, pl.ds(0, nx)], comp_send.at[0],
                comp_recv.at[s], {"chain": c},
            ).wait_recv()
            remote(
                back, back_in.at[s], back_send.at[0], back_recv.at[s], {"chain": c}
            ).wait_recv()
            return exact_dot_t(state, gathered[s, :nx]) + back_in[s]

        behind[count - 1] = lax.fori_loop(0, n - 1 - c, fold, jnp.zeros((columns, nx), F32))

    for p in reversed(range(count)):
        if p + 1 < count:
            @pl.when(is_owner)
            def _():
                behind[p] = exact_dot_t(behind[p + 1], summed[p + 1, :nx]) + carried_sum[p + 1]
        spread(behind, p, beh_send, beh_recv)

    for p in reversed(range(count)):
        @pl.when(jnp.logical_not(is_owner))
        def _():
            remote(
                behind.at[p], behind.at[p], beh_send.at[p, 0], beh_recv.at[p], {"col": k}
            ).wait_recv()
        out_ref[p] = applied[p] - split_dot_t(behind[p], following(p))

    for condition, args in unsent:
        @pl.when(condition)
        def _():
            remote(*args).wait_send()


def shards(n, m, rhs, block_inverse, entry_factor, exit_factor, previous):
    count, columns, width = rhs.shape
    nx = entry_factor.shape[2]
    padded = -(-width // 128) * 128
    if padded != width:
        extra = padded - width
        rhs = jnp.pad(rhs, ((0, 0), (0, 0), (0, extra)))
        previous = jnp.pad(previous, ((0, 0), (0, extra)))
        entry_factor = jnp.pad(entry_factor, ((0, 0), (0, extra), (0, 0)))
        exit_factor = jnp.pad(exit_factor, ((0, 0), (0, extra), (0, 0)))
        block_inverse = jnp.pad(
            block_inverse.reshape(count, width, m, width),
            ((0, 0), (0, extra), (0, 0), (0, extra)),
        ).reshape(count, padded, m * padded)
    vmem = pltpu.VMEM
    dma = pltpu.SemaphoreType.DMA
    out = pl.pallas_call(
        functools.partial(kernel, n, m),
        out_shape=jax.ShapeDtypeStruct((count, columns, padded), F32),
        in_specs=[pl.BlockSpec(memory_space=pl.ANY)] * 5,
        out_specs=pl.BlockSpec(memory_space=pltpu.VMEM),
        scratch_shapes=[
            vmem((count, columns, padded), BF16),
            vmem(block_inverse.shape, BF16),
            vmem(entry_factor.shape, BF16),
            vmem(exit_factor.shape, BF16),
            vmem(previous.shape, BF16),
            vmem(exit_factor.shape[1:], BF16),
            vmem((count, nx + columns, nx), F32),
            vmem((m, count, nx + columns, nx), F32),
            vmem((columns, nx), F32),
            vmem((m, columns, nx), F32),
            vmem((count, nx + columns, nx), F32),
            vmem((nx + columns, nx), F32),
            vmem((n, nx + columns, nx), F32),
            vmem((count, columns, nx), F32),
            vmem((m, count, columns, padded), BF16),
            vmem((count, columns, padded), F32),
            vmem((count, columns, nx), F32),
            vmem((m, count, columns, nx), F32),
            vmem((count, columns, nx), F32),
            vmem((columns, nx), F32),
            vmem((n, columns, nx), F32),
            vmem((count, columns, nx), F32),
            dma((4 + count,)),
            dma((2,)),
            dma((count,)), dma((m, count)),
            dma(()), dma((m,)),
            dma((2 * (n - 1),)), dma((n,)),
            dma((count, m - 1)), dma((count,)),
            dma((m, count, 2)), dma((m, count)),
            dma((count,)), dma((m, count)),
            dma((n - 1,)), dma((n,)),
            dma((count, m - 1)), dma((count,)),
        ],
        compiler_params=pltpu.CompilerParams(
            collective_id=0, has_side_effects=True, vmem_limit_bytes=48 * 1024 * 1024
        ),
    )(rhs, block_inverse, entry_factor, exit_factor, previous)
    return out[:, :, :width] if padded != width else out


def solution(mesh):
    placed = (
        P("chain", None, "col"),
        P("chain", "col", None),
        P("chain", "col", None),
        P("chain", "col", None),
        P(None, "col"),
    )
    return jax.shard_map(
        functools.partial(shards, mesh.shape["chain"], mesh.shape["col"]),
        mesh=mesh, in_specs=placed, out_specs=P("chain", None, "col"), check_vma=False,
    )
```

time: 162 us -> 56.7 us (0.35)
  blocking collectives: 76.4 us -> 0 us
  Pallas kernels: 0 us -> 52 us
  waiting for transfers between devices: 45 us -> 0 us
  matrix products: 22.7 us -> 0 us
  between operations: 13.6 us -> 0.01 us
  local copies, waits for them, and re-layouts: 1.46 us -> 4.47 us
    all_gather x5 -> x0, blocking collectives: 55.4 us -> none  [the longest x4 38.2 us: entering(): gathered = jax.tree.map(lambda a: lax.all_gather(a, axis), part)]
    pallas_call x0 -> x1, Pallas kernels: none -> 52 us  [shards(): pl.pallas_call(functools.partial(kernel, n, m), out_shape=jax.ShapeDtypeS...]
    psum x2 -> x0, waiting for transfers between devices: 43.2 us -> none  [the longest x1 24.6 us: shards(): carried = lax.psum(carried_part, 'col')]
    dot_general x27 -> x0, matrix products: 22.7 us -> none  [the longest x1 4.94 us: shards(): jnp.einsum('icb,irb->icr', lax.all_gather(forward, 'col', axis=2, tiled=T...]
    psum x1 -> x0, blocking collectives: 21 us -> none  [shards(): lax.psum((couple_part, source_part, opening_part), 'col')]
    unnamed x12 -> x9, local copies, waits for them, and re-layouts: 0.34 us -> 4.47 us
    ppermute x1 -> x0, waiting for transfers between devices: 1.82 us -> none  [from_behind(): return lax.ppermute(block, axis, route)]
  transfers between devices with their start and end apart: 3 -> 0, of which waited for: 3 -> 0; matrix products, arithmetic and copies ran while one was open for 1% -> 0% of each run, Pallas kernels for 0% -> 0%
where the time goes in v1:
time: 56.7 us; the launch traced here: 56.4 us
  Pallas kernels  52 us (92%)
  local copies, waits for them, and re-layouts  4.47 us (8%)
    pallas_call x1, Pallas kernels, shards(): pl.pallas_call(functools.partial(kernel, n, m), out_shape=jax.ShapeDtypeS...  52 us
    unnamed x9, local copies, waits for them, and re-layouts  4.47 us

profile of v1, /device:TPU:0, one launch (start us, length us, event | category | flops | bytes accessed | tf_op | source)
XLA Modules:
  0.0 56.4 jit_solution(7114028749270486861)
XLA Ops:
  0.0 0.0 copy-start
  0.0 1.0 %copy-done = bf16[2,640,128]{2,1,0:T(8,128)(2,1)S(1)} copy-done((bf16[2,640,128]{2,1,0:T(8,128)(2,1)S(1)}, bf16[2,640,128]{2,1,0:T(8,128)(2,1)}, u32[]{:S(2)}) %copy-start) | copy-done | bytes 327704
  1.0 0.0 copy-start.1
  1.0 1.0 %copy-done.1 = bf16[2,640,128]{2,1,0:T(8,128)(2,1)S(1)} copy-done((bf16[2,640,128]{2,1,0:T(8,128)(2,1)S(1)}, bf16[2,640,128]{2,1,0:T(8,128)(2,1)}, u32[]{:S(2)}) %copy-start.1) | copy-done | bytes 327704
  1.9 0.0 copy-start.2
  1.9 0.9 %copy-done.2 = bf16[2,64,640]{2,1,0:T(8,128)(2,1)S(1)} copy-done((bf16[2,64,640]{2,1,0:T(8,128)(2,1)S(1)}, bf16[2,64,640]{2,1,0:T(8,128)(2,1)}, u32[]{:S(2)}) %copy-start.2) | copy-done | bytes 163864
  2.9 0.0 copy-start.3
  2.9 0.9 %copy-done.3 = bf16[64,640]{1,0:T(8,128)(2,1)S(1)} copy-done((bf16[64,640]{1,0:T(8,128)(2,1)S(1)}, bf16[64,640]{1,0:T(8,128)(2,1)}, u32[]{:S(2)}) %copy-start.3) | copy-done | bytes 81944
  3.8 52.0 %shard_map.55 = f32[2,64,640]{2,1,0:T(8,128)S(1)} custom-call(bf16[2,64,640]{2,1,0:T(8,128)(2,1)S(1)} %copy-done.2, bf16[2,640,2560]{2,1,0:T(8,128)(2,1)} %binv_hbm.1, bf16[2,640,128]{2,1,0:T(8,128)(2,1)S(1)} %copy-done, bf16[2,640,128]{2,1,0:T(8,128)(2,1)S(1)} %copy-done.1, bf16[64,640]{1,0:T(8,128)(2,1)S(1)} %copy-done.3), custom_call_target="tpu_custom_call" | custom-call | tf_op jit(solution)/shard_map/pallas_call | solution.py:365
  55.7 0.7 %copy.7 = f32[2,64,640]{2,1,0:T(8,128)} copy(f32[2,64,640]{2,1,0:T(8,128)S(1)} %shard_map.55) | data formatting | bytes 655360
Async XLA Ops:
  0.0 1.0 %copy-start = (bf16[2,640,128]{2,1,0:T(8,128)(2,1)S(1)}, bf16[2,640,128]{2,1,0:T(8,128)(2,1)}, u32[]{:S(2)}) copy-start(bf16[2,640,128]{2,1,0:T(8,128)(2,1)} %entry_hbm.1) | copy-start | bytes 983044
  1.0 1.0 %copy-start.1 = (bf16[2,640,128]{2,1,0:T(8,128)(2,1)S(1)}, bf16[2,640,128]{2,1,0:T(8,128)(2,1)}, u32[]{:S(2)}) copy-start(bf16[2,640,128]{2,1,0:T(8,128)(2,1)} %exit_hbm.1) | copy-start | bytes 983044
  1.9 0.9 %copy-start.2 = (bf16[2,64,640]{2,1,0:T(8,128)(2,1)S(1)}, bf16[2,64,640]{2,1,0:T(8,128)(2,1)}, u32[]{:S(2)}) copy-start(bf16[2,64,640]{2,1,0:T(8,128)(2,1)} %rhs_hbm.1) | copy-start | bytes 491524
  2.9 0.9 %copy-start.3 = (bf16[64,640]{1,0:T(8,128)(2,1)S(1)}, bf16[64,640]{1,0:T(8,128)(2,1)}, u32[]{:S(2)}) copy-start(bf16[64,640]{1,0:T(8,128)(2,1)} %prev_hbm.1) | copy-start | bytes 245764

commit v2 on v1

--- a/solution.py
+++ b/solution.py
@@ -30,27 +30,23 @@
     return (product[2 * rows:] + product[rows:2 * rows]) + product[:rows]
 
 
-def wide_dot(a, b, dot):
-    rows = a.shape[0]
+def exact_dot(a, b):
     a1, a2, a3 = terms(a)
     b1, b2, b3 = terms(b)
-    p1 = dot(jnp.concatenate([a1, a2, a3], axis=0), b1)
-    p2 = dot(jnp.concatenate([a1, a2], axis=0), b2)
-    p3 = dot(a1, b3)
-    small = (p1[2 * rows:] + p2[rows:]) + p3
-    return (small + (p1[rows:2 * rows] + p2[:rows])) + p1[:rows]
-
-
-def plain_dot(a, b):
-    return jnp.dot(a, b, preferred_element_type=F32)
-
-
-def exact_dot(a, b):
-    return wide_dot(a, b, plain_dot)
+    return jnp.dot(
+        jnp.concatenate([a3, a2, a1, a2, a1, a1], axis=1),
+        jnp.concatenate([b1, b2, b3, b1, b2, b1], axis=0),
+        preferred_element_type=F32,
+    )
 
 
 def exact_dot_t(a, b):
-    return wide_dot(a, b, dot_t)
+    a1, a2, a3 = terms(a)
+    b1, b2, b3 = terms(b)
+    return dot_t(
+        jnp.concatenate([a3, a2, a1, a2, a1, a1], axis=1),
+        jnp.concatenate([b1, b2, b3, b1, b2, b1], axis=1),
+    )
 
 
 def kernel(
@@ -126,25 +122,33 @@
     def _():
         arriving[...] = jnp.zeros_like(arriving)
 
+    for load in loads[:4]:
+        load.wait()
+
+    @pl.when(c == 0)
+    def _():
+        opening[...] = jnp.dot(prev[...], exits[0], preferred_element_type=F32)
+
+    def following(p):
+        return exits[p + 1] if p + 1 < count else arriving[...]
+
+    def part(p):
+        parts[p, :nx] = -lax.dot_general(
+            entry[p], following(p), (((0,), (0,)), ((), ())), preferred_element_type=F32
+        )
+        parts[p, nx:] = jnp.dot(rhs[p], following(p), preferred_element_type=F32)
+
+    for p in range(count - 1):
+        part(p)
+
     expected = m - 1 + jnp.where(c > 0, 1, 0) + jnp.where(c < n - 1, 1, 0)
     pl.semaphore_wait(barrier, expected + jnp.where(is_owner, n - 1, 0))
 
-    loads[0].wait()
     send(c > 0, exits.at[0], arriving, exit_sem.at[0], exit_sem.at[1], {"chain": c - 1})
-    for load in loads[1:4]:
-        load.wait()
-
-    @pl.when(c == 0)
-    def _():
-        opening[...] = jnp.dot(prev[...], exits[0], preferred_element_type=F32)
-
     send(
         (c == 0) & jnp.logical_not(is_owner), opening, opening_in.at[k],
         open_send, open_recv.at[k], {"col": owner},
     )
-
-    def following(p):
-        return exits[p + 1] if p + 1 < count else arriving[...]
 
     for p in range(count):
         if p + 1 == count:
@@ -153,10 +157,7 @@
                 remote(
                     exits.at[0], arriving, exit_sem.at[0], exit_sem.at[1], {"chain": c}
                 ).wait_recv()
-        parts[p, :nx] = -lax.dot_general(
-            entry[p], following(p), (((0,), (0,)), ((), ())), preferred_element_type=F32
-        )
-        parts[p, nx:] = jnp.dot(rhs[p], following(p), preferred_element_type=F32)
+            part(p)
         send(
             jnp.logical_not(is_owner), parts.at[p], parts_in.at[k, p],
             part_send.at[p], part_recv.at[k, p], {"col": owner},
@@ -203,9 +204,14 @@
 
     for d in range(1, n):
         later = lax.rem(c + d, n)
+        there = {"chain": later, "col": owner_of(later)}
         send(
-            is_owner & (c + d < n), comp, gathered.at[c], comp_send.at[d - 1],
-            comp_recv.at[c], {"chain": later, "col": owner_of(later)},
+            is_owner & (c > 0) & (c + d < n), comp, gathered.at[c], comp_send.at[d - 1],
+            comp_recv.at[c], there,
+        )
+        send(
+            is_owner & (c == 0), comp.at[pl.ds(nx, columns)],
+            gathered.at[c, pl.ds(nx, columns)], comp_send.at[d - 1], comp_recv.at[c], there,
         )
     for d in range(1, n):
         earlier = lax.rem(c - d + n, n)
@@ -223,7 +229,11 @@
             ).wait_recv()
             return exact_dot(state, gathered[s, :nx]) + gathered[s, nx:]
 
-        states[0] = lax.fori_loop(0, c, fold, jnp.zeros((columns, nx), F32))
+        remote(
+            comp.at[pl.ds(nx, columns)], gathered.at[0, pl.ds(nx, columns)],
+            comp_send.at[0], comp_recv.at[0], {"chain": c},
+        ).wait_recv()
+        states[0] = lax.fori_loop(1, c, fold, gathered[0, nx:])
 
     for p in range(count):
         if p > 0:
@@ -269,20 +279,24 @@
                     ).wait_recv()
 
                 send(
-                    there & (beyond >= 0) & (beyond < m), forward.at[j, p], forward.at[j, p],
+                    there & (beyond >= 0) & (beyond < m),
+                    forward.at[j, p], forward.at[j, p],
                     fwd_send.at[j, p, way], fwd_recv.at[j, p], {"col": beyond},
                 )
-
-                @pl.when(there)
+            for step in (1, -1):
+                j = k - step * d
+
+                @pl.when((j >= 0) & (j < m))
                 def _():
                     applied[p] += dot_t(forward[j, p], block(j, p))
-
-    for p in reversed(range(count)):
-        carried[p] = jnp.dot(applied[p].astype(BF16), entry[p], preferred_element_type=F32)
-        send(
-            jnp.logical_not(is_owner), carried.at[p], carried_in.at[k, p],
-            car_send.at[p], car_recv.at[k, p], {"col": owner},
-        )
+            if d == m - 1:
+                carried[p] = jnp.dot(
+                    applied[p].astype(BF16), entry[p], preferred_element_type=F32
+                )
+                send(
+                    jnp.logical_not(is_owner), carried.at[p], carried_in.at[k, p],
+                    car_send.at[p], car_recv.at[k, p], {"col": owner},
+                )
 
     @pl.when(is_owner)
     def _():
@@ -402,7 +416,7 @@
             dma((count, m - 1)), dma((count,)),
         ],
         compiler_params=pltpu.CompilerParams(
-            collective_id=0, has_side_effects=True, vmem_limit_bytes=48 * 1024 * 1024
+            collective_id=0, has_side_effects=True
         ),
     )(rhs, block_inverse, entry_factor, exit_factor, previous)
     return out[:, :, :width] if padded != width else out

time: 56.7 us -> 52.7 us (0.929)
  local copies, waits for them, and re-layouts: 4.47 us -> 1.72 us
  Pallas kernels: 52 us -> 50.8 us
    unnamed x9 -> x1, local copies, waits for them, and re-layouts: 4.47 us -> 1.72 us
    pallas_call x1, Pallas kernels: 52 us -> 50.8 us  [shards(): pl.pallas_call(functools.partial(kernel, n, m), out_shape=jax.ShapeDtypeS...]
where the time goes in v2:
time: 52.7 us; the launch traced here: 52.5 us
  Pallas kernels  50.8 us (96%)
  local copies, waits for them, and re-layouts  1.72 us (3%)
    pallas_call x1, Pallas kernels, shards(): pl.pallas_call(functools.partial(kernel, n, m), out_shape=jax.ShapeDtypeS...  50.8 us
    unnamed x1, local copies, waits for them, and re-layouts  1.72 us

profile of v2, /device:TPU:0, one launch (start us, length us, event | category | flops | bytes accessed | tf_op | source)
XLA Modules:
  0.0 52.5 jit_solution(15911800497280176965)
XLA Ops:
  0.0 50.8 %shard_map.55 = f32[2,64,640]{2,1,0:T(8,128)} custom-call(bf16[2,64,640]{2,1,0:T(8,128)(2,1)} %rhs_hbm.1, bf16[2,640,2560]{2,1,0:T(8,128)(2,1)} %binv_hbm.1, bf16[2,640,128]{2,1,0:T(8,128)(2,1)} %entry_hbm.1, bf16[2,640,128]{2,1,0:T(8,128)(2,1)} %exit_hbm.1, bf16[64,640]{1,0:T(8,128)(2,1)} %prev_hbm.1), custom_call_target="tpu_custom_call" | custom-call | tf_op jit(solution)/shard_map/pallas_call | solution.py:379
  50.8 1.7 %copy.7 = f32[2,64,640]{2,1,0:T(8,128)} copy(f32[2,64,640]{2,1,0:T(8,128)} %shard_map.55) | data formatting | bytes 655360
